TPU v7x, 16 devices: a whole 2x2x2 slice. The times are simulated.
16 devices in a mesh: rep: 1, r: 2 (over z), s: 8 (over x, y, core).
Axes of the slice: x: 2, y: 2, z: 2, core: 2. Of those that a mesh axis runs over, the one named last changes fastest.
Arguments:
- x: bfloat16 [16, 4096, 896], P(('rep', 'r', 's'))
- dy: bfloat16 [16, 4096, 896], P(('rep', 'r', 's'))
- w_gate: bfloat16 [2, 896, 2304], P(None, 's')
- w_up: bfloat16 [2, 896, 2304], P(None, 's')
- w_down: bfloat16 [2, 2304, 896], P(None, 's')
- m_w_gate: float32 [2, 896, 2304], P(None, 's')
- m_w_up: float32 [2, 896, 2304], P(None, 's')
- m_w_down: float32 [2, 2304, 896], P(None, 's')
- v_w_gate: float32 [2, 896, 2304], P(None, 's')
- v_w_up: float32 [2, 896, 2304], P(None, 's')
- v_w_down: float32 [2, 2304, 896], P(None, 's')
Outputs:
- output 1: bfloat16 [2, 896, 2304], P('rep', 's')
- output 2: bfloat16 [2, 896, 2304], P('rep', 's')
- output 3: bfloat16 [2, 2304, 896], P('rep', 's')
- output 4: float32 [2, 896, 2304], P('rep', 's')
- output 5: float32 [2, 896, 2304], P('rep', 's')
- output 6: float32 [2, 2304, 896], P('rep', 's')
- output 7: float32 [2, 896, 2304], P('rep', 's')
- output 8: float32 [2, 896, 2304], P('rep', 's')
- output 9: float32 [2, 2304, 896], P('rep', 's')
All inputs are finite; a program needn't handle non-finite values.
Results may differ from a plain program's by a relative error of at most 0.022.
Values are sent between devices in bfloat16 or wider.
A program may use at most 2 GiB of HBM per device.

v0:
```python
import functools

import jax
import jax.numpy as jnp
from jax import lax
from jax.experimental import pallas as pl
from jax.experimental.pallas import tpu as pltpu
from jax.sharding import PartitionSpec as P

NAMES = ("w_gate", "w_up", "w_down")
MESH = pl.DeviceIdType.MESH
BF, F32 = jnp.bfloat16, jnp.float32
LIMIT = 60 * 1024 * 1024
LANES = 128


def wide(a):
    return a.astype(F32)


def dot(a, b, contract=((1,), (0,))):
    return lax.dot_general(a, b, (contract, ((), ())), preferred_element_type=F32)


def scale_of(h):
    return lax.rsqrt(jnp.mean(h * h, -1, keepdims=True) + 1e-6)


class Place:
    def __init__(self):
        s = lax.axis_index("s")
        x, y, core = s // 4, (s // 2) % 2, s % 2
        at = lambda x, y, core: x * 4 + y * 2 + core
        self.s, self.z = s, lax.axis_index("r")
        self.other, self.xn, self.yn, self.diagonal = at(x, y, 1 - core), at(1 - x, y, core), at(x, 1 - y, core), at(1 - x, 1 - y, core)

    def neighbours(self):
        return ({"s": self.other}, {"s": self.xn}, {"s": self.yn}, {"r": 1 - self.z})

    def barrier(self):
        barrier = pltpu.get_barrier_semaphore()
        for device in self.neighbours():
            pl.semaphore_signal(barrier, inc=1, device_id=device, device_id_type=MESH)
        pl.semaphore_wait(barrier, 4)


TRANSFERS = 13


class Gather:
    def __init__(self, place, block, whole, split, sems):
        self.p, self.block, self.whole = place, block, whole
        self.rows = block.shape[0]
        self.axis, first, second = split
        self.parts = ((0, first), (first, second))
        self.half = first + second
        self.send, self.recv, self.local = sems

    def at(self, s):
        return self.whole.at[pl.ds(pl.multiple_of(s * self.rows, 16), self.rows)]

    def part(self, s, z, which):
        start, size = self.parts[which]
        offset = z * self.half + start
        if self.axis == 1:
            return self.at(s).at[:, pl.ds(pl.multiple_of(offset, LANES), size)]
        return self.whole.at[pl.ds(pl.multiple_of(s * self.rows + offset, 16), size)]

    def copy(self, k):
        p, z = self.p, self.p.z
        core, xn, yn, zn = self.p.neighbours()
        source, target, device = {
            0: lambda: (self.block, self.at(p.s), core),
            1: lambda: (self.block, self.at(p.s), xn),
            2: lambda: (self.block, self.at(p.s), yn),
            3: lambda: (self.at(p.xn), self.at(p.xn), core),
            4: lambda: (self.at(p.yn), self.at(p.yn), core),
            5: lambda: (self.part(p.xn, z, 0), self.part(p.xn, z, 0), yn),
            6: lambda: (self.part(p.yn, z, 1), self.part(p.yn, z, 1), xn),
            7: lambda: (self.part(p.diagonal, z, 0), self.part(p.diagonal, z, 0), zn),
            8: lambda: (self.part(p.diagonal, z, 1), self.part(p.diagonal, z, 1), zn),
            9: lambda: (self.part(p.diagonal, z, 0), self.part(p.diagonal, z, 0), core),
            10: lambda: (self.part(p.diagonal, z, 1), self.part(p.diagonal, z, 1), core),
            11: lambda: (self.part(p.diagonal, 1 - z, 0), self.part(p.diagonal, 1 - z, 0), core),
            12: lambda: (self.part(p.diagonal, 1 - z, 1), self.part(p.diagonal, 1 - z, 1), core),
        }[k]()
        return pltpu.make_async_remote_copy(
            src_ref=source, dst_ref=target, send_sem=self.send.at[k], recv_sem=self.recv.at[k], device_id=device, device_id_type=MESH
        )

    def keep(self):
        return pltpu.make_async_copy(self.block, self.at(self.p.s), self.local)

    def start(self):
        for k in (1, 2, 0):
            self.copy(k).start()
        self.keep().start()

    def passing(self, after, then):
        self.copy(after).wait_recv()
        for k in then:
            self.copy(k).start()

    def second(self):
        self.passing(1, (5, 3))
        self.passing(2, (6, 4))

    def third(self):
        self.passing(5, (7, 9))
        self.passing(6, (8, 10))

    def fourth(self):
        self.passing(7, (11,))
        self.passing(8, (12,))

    def finish(self):
        for k in (0, 3, 4, 9, 10, 11, 12):
            self.copy(k).wait_recv()
        for k in range(TRANSFERS):
            self.copy(k).wait_send()
        self.keep().wait()


def gather_sems(jobs):
    return [pltpu.SemaphoreType.DMA((jobs, TRANSFERS)), pltpu.SemaphoreType.DMA((jobs, TRANSFERS)), pltpu.SemaphoreType.DMA((jobs,))]


def halves_of(columns):
    half = columns // 2
    first = (half // LANES + 1) // 2 * LANES
    return first, half - first


def on(step, *actions):
    @pl.when(step)
    def _():
        for action in actions:
            action()


def sigmoid(x):
    return 0.5 * jnp.tanh(0.5 * x) + 0.5


def gate_up_kernel(parts, tiles, h_ref, wg_ref, wu_ref, wd_ref, g_ref, u_ref, hid_ref, at_ref, wd0_ref, wg1_ref, wu1_ref, wg, wu, send, recv, local):
    part, tile = pl.program_id(0), pl.program_id(1)
    step = part * tiles + tile
    place = Place()
    width = g_ref.shape[1]
    sems = lambda j: (send.at[j], recv.at[j], local.at[j])
    jobs = []
    for n in range(parts):
        cols = pl.ds(n * width, width)
        for i, (own, whole) in enumerate(((wg_ref, wg), (wu_ref, wu))):
            jobs.append(Gather(place, own.at[0, :, cols], whole.at[:, cols], (1, *halves_of(width)), sems(2 * n + i)))
    rows = wd_ref.shape[1]
    down = Gather(place, wd_ref.at[0], wd0_ref, (0, (rows // 2 // 16 + 1) // 2 * 16, rows // 2 - (rows // 2 // 16 + 1) // 2 * 16), sems(2 * parts))
    gate1 = Gather(place, wg_ref.at[1], wg1_ref, (1, *halves_of(wg_ref.shape[2])), sems(2 * parts + 1))
    up1 = Gather(place, wu_ref.at[1], wu1_ref, (1, *halves_of(wu_ref.shape[2])), sems(2 * parts + 2))
    b = lambda n, what: [getattr(jobs[2 * n + i], what) for i in range(2)]
    last = parts * tiles - 1

    on(
        step == 0,
        place.barrier,
        *b(0, "start"),
        *b(0, "second"),
        *b(1, "start"),
        *b(0, "third"),
        *b(0, "fourth"),
        *b(0, "finish"),
        *b(1, "second"),
        *b(2, "start"),
    )
    on(step == 2, *b(1, "third"))
    on(step == 3, *b(1, "fourth"))
    on(step == 4, down.start)
    on(step == 5, *b(2, "second"))
    on(step == 7, *b(2, "third"))
    on(step == 8, *b(1, "finish"))
    on(step == 9, *b(2, "fourth"), gate1.start)
    on(step == 11, down.second)
    on(step == 13, down.third)
    on(step == 14, up1.start)
    on(step == 15, down.fourth)
    on(step == 16, *b(2, "finish"))
    on(step == 17, gate1.second, down.finish)
    on(step == 19, gate1.third)
    on(step == 21, gate1.fourth)
    on(step == 22, up1.second, gate1.finish)

    h = wide(h_ref[...])
    a = (h * scale_of(h)).astype(BF)

    @pl.when(part == 0)
    def _():
        at_ref[...] = a.T

    for n in range(0, width, 256):
        where = pl.ds(pl.multiple_of(part * width + n, LANES), 256)
        g = dot(a, wg[:, where])
        u = dot(a, wu[:, where])
        g_ref[:, n : n + 256] = g
        u_ref[:, n : n + 256] = u
        hid_ref[:, n : n + 256] = (g * sigmoid(g) * u).astype(BF)

    on(step == last, up1.third, up1.fourth, up1.finish)


def gate_up(h, wg, wu, wd):
    tokens, d = h.shape
    _, rows, f = wg.shape
    parts, tile = 3, 512
    width, tiles = f // parts, tokens // tile
    group = d // rows
    any_ = pl.BlockSpec(memory_space=pl.ANY)
    return pl.pallas_call(
        functools.partial(gate_up_kernel, parts, tiles),
        grid=(parts, tiles),
        out_shape=[
            jax.ShapeDtypeStruct((tokens, f), F32),
            jax.ShapeDtypeStruct((tokens, f), F32),
            jax.ShapeDtypeStruct((tokens, f), BF),
            jax.ShapeDtypeStruct((d, tokens), BF),
            jax.ShapeDtypeStruct((wd.shape[1] * group, d), BF),
            jax.ShapeDtypeStruct((d, f), BF),
            jax.ShapeDtypeStruct((d, f), BF),
        ],
        in_specs=[pl.BlockSpec((tile, d), lambda p, t: (t, 0)), any_, any_, any_],
        out_specs=[pl.BlockSpec((tile, width), lambda p, t: (t, p))] * 3
        + [pl.BlockSpec((d, tile), lambda p, t: (0, jnp.where(p == 0, t, tiles - 1))), any_, any_, any_],
        scratch_shapes=[pltpu.VMEM((d, f), BF)] * 2 + gather_sems(2 * parts + 3),
        compiler_params=pltpu.CompilerParams(
            collective_id=0, has_side_effects=True, vmem_limit_bytes=LIMIT, dimension_semantics=("arbitrary", "arbitrary")
        ),
        cost_estimate=pl.CostEstimate(flops=4 * tokens * d * f, bytes_accessed=110_000_000, transcendentals=tokens * f),
        name="gate_up",
    )(h, wg, wu, wd)


def down_kernel(tiles, hid_ref, h_ref, w_ref, wd_ref, h1_ref, wd1_ref, send, recv, local):
    step = pl.program_id(0)
    place = Place()
    sems = lambda j: (send.at[j], recv.at[j], local.at[j])
    rows = wd_ref.shape[1]
    down = Gather(place, wd_ref.at[1], wd1_ref, (0, (rows // 2 // 16 + 1) // 2 * 16, rows // 2 - (rows // 2 // 16 + 1) // 2 * 16), sems(0))
    on(step == 0, place.barrier, down.start)
    on(step == tiles // 2 + 1, down.second)
    on(step == tiles // 2 + 2, down.third)
    h1_ref[...] = h_ref[...] + dot(hid_ref[...], w_ref[...]).astype(BF)
    on(step == tiles - 1, down.fourth, down.finish)


def down(hid, h, w, wd):
    tokens, d = h.shape
    f = hid.shape[1]
    tile = 512
    any_ = pl.BlockSpec(memory_space=pl.ANY)
    return pl.pallas_call(
        functools.partial(down_kernel, tokens // tile),
        grid=(tokens // tile,),
        out_shape=[jax.ShapeDtypeStruct((tokens, d), BF), jax.ShapeDtypeStruct((f, d), BF)],
        in_specs=[
            pl.BlockSpec((tile, f), lambda t: (t, 0)),
            pl.BlockSpec((tile, d), lambda t: (t, 0)),
            pl.BlockSpec((f, d), lambda t: (0, 0), pipeline_mode=pl.Buffered(1)),
            any_,
        ],
        out_specs=[pl.BlockSpec((tile, d), lambda t: (t, 0)), any_],
        scratch_shapes=gather_sems(1),
        compiler_params=pltpu.CompilerParams(collective_id=1, has_side_effects=True, vmem_limit_bytes=LIMIT, dimension_semantics=("arbitrary",)),
        cost_estimate=pl.CostEstimate(flops=2 * tokens * d * f, bytes_accessed=37_000_000, transcendentals=0),
        name="down",
    )(hid, h, w, wd)


def last_kernel(h_ref, dy_ref, wg_ref, wu_ref, wd_ref, hid_ref, dg_ref, du_ref, at_ref, dyt_ref, dh_ref, dht_ref):
    h = wide(h_ref[...])
    scale = scale_of(h)
    a = (h * scale).astype(BF)
    dy = dy_ref[...]
    at_ref[...] = a.T
    dyt_ref[...] = dy.T
    f = wg_ref.shape[1]
    by_a = jnp.zeros(h.shape, F32)
    for n in range(0, f, 768):
        for k in range(n, n + 768, 256):
            where = slice(k, k + 256)
            g = dot(a, wg_ref[:, where])
            u = dot(a, wu_ref[:, where])
            back = wide(dot(dy, wd_ref[where, :], ((1,), (1,))).astype(BF))
            s = sigmoid(g)
            silu = g * s
            hid_ref[:, where] = (silu * u).astype(BF)
            du_ref[:, where] = (back * silu).astype(BF)
            dg_ref[:, where] = (back * u * (s * (1.0 + g * (1.0 - s)))).astype(BF)
        where = slice(n, n + 768)
        by_a += dot(dg_ref[:, where], wg_ref[:, where], ((1,), (1,))) + dot(du_ref[:, where], wu_ref[:, where], ((1,), (1,)))
    by_a = wide(by_a.astype(BF))
    mean = jnp.mean(by_a * h, -1, keepdims=True)
    by_h = (by_a * scale - h * (scale * scale * scale * mean)).astype(BF)
    by_h = dy + by_h
    dh_ref[...] = by_h
    dht_ref[...] = by_h.T


def last_layer(h, dy, wg, wu, wd):
    tokens, d = h.shape
    f = wg.shape[1]
    tile = 512
    rows = lambda n: pl.BlockSpec((tile, n), lambda t: (t, 0))
    columns = pl.BlockSpec((d, tile), lambda t: (0, t))
    fixed = lambda m, n: pl.BlockSpec((m, n), lambda t: (0, 0), pipeline_mode=pl.Buffered(1))
    shape = lambda *s: jax.ShapeDtypeStruct(s, BF)
    return pl.pallas_call(
        last_kernel,
        grid=(tokens // tile,),
        out_shape=[shape(tokens, f)] * 3 + [shape(d, tokens)] * 2 + [shape(tokens, d), shape(d, tokens)],
        in_specs=[rows(d), rows(d), fixed(d, f), fixed(d, f), fixed(f, d)],
        out_specs=[rows(f)] * 3 + [columns] * 2 + [rows(d), columns],
        compiler_params=pltpu.CompilerParams(vmem_limit_bytes=LIMIT, dimension_semantics=("arbitrary",)),
        cost_estimate=pl.CostEstimate(flops=10 * tokens * d * f, bytes_accessed=110_000_000, transcendentals=tokens * f),
        name="last_layer",
    )(h, dy, wg, wu, wd)


def back_kernel(dh_ref, g_ref, u_ref, wd_ref, dg_ref, du_ref):
    dh = dh_ref[...]
    for k in range(0, g_ref.shape[1], 256):
        where = slice(k, k + 256)
        back = wide(dot(dh, wd_ref[where, :], ((1,), (1,))).astype(BF))
        g, u = g_ref[:, where], u_ref[:, where]
        s = sigmoid(g)
        du_ref[:, where] = (back * (g * s)).astype(BF)
        dg_ref[:, where] = (back * u * (s * (1.0 + g * (1.0 - s)))).astype(BF)


def back_to_hidden(dh, g, u, wd):
    tokens, d = dh.shape
    f = g.shape[1]
    tile = 512
    rows = lambda n: pl.BlockSpec((tile, n), lambda t: (t, 0))
    return pl.pallas_call(
        back_kernel,
        grid=(tokens // tile,),
        out_shape=[jax.ShapeDtypeStruct((tokens, f), BF)] * 2,
        in_specs=[rows(d), rows(f), rows(f), pl.BlockSpec((f, d), lambda t: (0, 0), pipeline_mode=pl.Buffered(1))],
        out_specs=[rows(f)] * 2,
        compiler_params=pltpu.CompilerParams(vmem_limit_bytes=LIMIT, dimension_semantics=("arbitrary",)),
        cost_estimate=pl.CostEstimate(flops=2 * tokens * d * f, bytes_accessed=125_000_000, transcendentals=tokens * f),
        name="back_to_hidden",
    )(dh, g, u, wd)


class Sum:
    COPIES = 7

    def __init__(self, place, store, out, squares, columns, x_first, send, recv):
        self.p, self.out, self.squares, self.x_first = place, out, squares, x_first
        self.term, self.rc, self.sx, self.rx, self.sy, self.ry, self.sz, self.rz = store
        self.rows = self.term.shape[0] // 8
        self.c0, self.width = columns
        self.cols = pl.ds(self.c0, self.width)
        self.send, self.recv = send, recv
        s = place.s
        self.x, self.y, self.core = s // 4, (s // 2) % 2, s % 2

    def chip(self, near, far):
        return near * 2 + far if self.x_first else far * 2 + near

    def block(self, chip, core):
        return pl.ds(pl.multiple_of((chip * 2 + core) * self.rows, 16), self.rows)

    def copy(self, k):
        core, xn, yn, zn = self.p.neighbours()
        first, second = (xn, yn) if self.x_first else (yn, xn)
        if k < 4:
            source, target, device = self.term.at[self.block(k, 1 - self.core), self.cols], self.rc.at[k, :, self.cols], core
        elif k == 4:
            source, target, device = self.sx.at[:, :, self.cols], self.rx.at[:, :, self.cols], first
        elif k == 5:
            source, target, device = self.sy.at[:, self.cols], self.ry.at[:, self.cols], second
        else:
            source, target, device = self.sz.at[:, self.cols], self.rz.at[:, self.cols], zn
        return pltpu.make_async_remote_copy(
            src_ref=source, dst_ref=target, send_sem=self.send.at[k], recv_sem=self.recv.at[k], device_id=device, device_id_type=MESH
        )

    def mine(self, chip, r):
        start = pl.multiple_of((chip * 2 + self.core) * self.rows + r * 16, 16)
        return wide(self.term[pl.ds(start, 16), self.cols]) + wide(self.rc[chip, pl.ds(pl.multiple_of(r * 16, 16), 16), self.cols])

    def each(self, body):
        def go(r, carry):
            body(r, pl.ds(pl.multiple_of(r * 16, 16), 16))
            return carry

        lax.fori_loop(0, self.rows // 16, go, 0)

    def stage0(self):
        for k in range(4):
            self.copy(k).start()

    def stage1(self):
        for k in range(4):
            self.copy(k).wait_recv()
        near = (1 - self.x) if self.x_first else (1 - self.y)

        def body(r, rows):
            for far in range(2):
                self.sx[far, rows, self.cols] = self.mine(self.chip(near, far), r).astype(BF)

        self.each(body)
        self.copy(4).start()

    def stage2(self):
        self.copy(4).wait_recv()
        near, far = (self.x, 1 - self.y) if self.x_first else (self.y, 1 - self.x)

        def body(r, rows):
            self.sy[rows, self.cols] = (self.mine(self.chip(near, far), r) + wide(self.rx[far, rows, self.cols])).astype(BF)

        self.each(body)
        self.copy(5).start()

    def stage3(self):
        self.copy(5).wait_recv()
        for k in range(4):
            self.copy(k).wait_send()
        near, far = (self.x, self.y) if self.x_first else (self.y, self.x)

        def body(r, rows):
            total = self.mine(self.chip(near, far), r) + wide(self.rx[far, rows, self.cols]) + wide(self.ry[rows, self.cols])
            self.sz[rows, self.cols] = total.astype(BF)

        self.each(body)
        self.copy(6).start()

    def stage4(self):
        self.copy(6).wait_recv()

        def body(r, rows):
            total = (wide(self.sz[rows, self.cols]) + wide(self.rz[rows, self.cols])).astype(BF)
            self.out[rows, self.cols] = total
            square = wide(total) * wide(total)
            square = square[:8] + square[8:]
            part = square[:, :LANES]
            for k in range(LANES, self.width, LANES):
                part = part + square[:, k : k + LANES]
            self.squares[...] += part

        self.each(body)
        for k in range(4, self.COPIES):
            self.copy(k).wait_send()


TILE = 256


def gradients_kernel(phases, pieces, tiles, *refs):
    lefts, rights = refs[:4], refs[4:10]
    outs, total_ref = refs[10:16], refs[16]
    left, right, l_sem, r_sem, *rest = refs[17:]
    stores = [rest[8 * i : 8 * i + 8] for i in range(3)]
    squares, parts, send, recv, psend, precv, free = rest[24:]
    place = Place()
    s, z = place.s, place.z
    barrier = pltpu.get_barrier_semaphore()
    peers = [(s + k) % 8 for k in range(1, 8)]
    for peer in peers:
        pl.semaphore_signal(barrier, inc=1, device_id={"s": peer}, device_id_type=MESH)
    pl.semaphore_signal(barrier, inc=1, device_id={"r": 1 - z}, device_id_type=MESH)
    pl.semaphore_wait(barrier, 8)

    sums = [Sum(place, stores[p["store"]], outs[p["phase"]], squares, p["columns"], p["x_first"], send.at[q], recv.at[q]) for q, p in enumerate(pieces)]
    neighbours = place.neighbours()

    def give(pair):
        for d, device in enumerate(neighbours):
            pl.semaphore_signal(free.at[pair, d], inc=1, device_id=device, device_id_type=MESH)

    def take(pair):
        for d in range(4):
            pl.semaphore_wait(free.at[pair, d], 1)

    def load_left(k):
        return pltpu.make_async_copy(lefts[k], left.at[k % 2], l_sem.at[k % 2])

    def load_right(phase, i, slot):
        cols = pl.ds(pl.multiple_of(i * TILE, TILE), TILE)
        return pltpu.make_async_copy(rights[phase].at[:, cols], right.at[slot], r_sem.at[slot])

    squares[...] = jnp.zeros_like(squares)
    load_left(0).start()
    load_right(0, 0, 0).start()
    load_left(1).start()
    load_right(0, 1, 1).start()
    at = {}
    for q, p in enumerate(pieces):
        for stage, step in enumerate(p["steps"]):
            at.setdefault(step, []).append((q, stage))

    def run(q, stage):
        p = pieces[q]
        if stage == 0 and p["take"] is not None:
            take(p["take"])
        getattr(sums[q], f"stage{stage}")()
        if stage == 4 and p["give"] is not None:
            give(p["give"])

    slots = 2
    for n, (which, turned, store, loads) in enumerate(phases):
        if n == 0 or phases[n - 1][0] != which:
            load_left(which).wait()
        if loads is not None:
            load_left(loads).start()
        term = stores[store][0]

        def tile(i, carry, n=n, which=which, turned=turned, term=term):
            for k in range(tiles):
                if n * tiles + k in at:
                    on(i == k, *[functools.partial(run, q, stage) for q, stage in at[n * tiles + k]])
            slot = (n * tiles + i) % slots
            load_right(n, i, slot).wait()
            total = dot(left[which % 2], right[slot])
            where = pl.ds(pl.multiple_of(i * TILE, TILE), TILE)
            if turned:
                term[where, :] = total.T.astype(BF)
            else:
                term[:, where] = total.astype(BF)

            @pl.when(i + slots < tiles)
            def _():
                load_right(n, i + slots, slot).start()

            if n + 1 < len(phases):

                @pl.when(i + slots >= tiles)
                def _():
                    load_right(n + 1, i + slots - tiles, slot).start()

            return carry

        lax.fori_loop(0, tiles, tile, 0)

    for step in sorted(at):
        if step >= len(phases) * tiles:
            for q, stage in at[step]:
                run(q, stage)

    def share(k):
        return pltpu.make_async_remote_copy(
            src_ref=squares,
            dst_ref=parts.at[s],
            send_sem=psend.at[k - 1],
            recv_sem=precv.at[k - 1],
            device_id={"s": peers[k - 1]},
            device_id_type=MESH,
        )

    for k in range(1, 8):
        share(k).start()
    parts[s] = squares[...]
    for k in range(1, 8):
        share(k).wait()
    total = parts[0]
    for k in range(1, 8):
        total = total + parts[k]
    total_ref[...] = total


def gradients(lefts, rights):
    d, tokens = lefts[0].shape
    f = rights[0].shape[1]
    tiles = f // TILE
    phases = [(0, True, 2, None), (1, False, 0, 2), (1, False, 1, None), (2, True, 2, 3), (3, False, 0, None), (3, False, 1, None)]
    gives, takes = {0: 2, 1: 0, 2: 1}, {3: 2, 4: 0, 5: 1}
    pieces = []
    for phase, (_, turned, store_of, _) in enumerate(phases):
        final = phase == len(phases) - 1
        columns = d if turned else f
        cuts = [0, 3 * TILE, 6 * TILE, columns - 3 * LANES, columns] if final else [0, -(-columns // 2 // LANES) * LANES, columns]
        gaps = (0, 2, 6, 9, 12) if final else (0, 2, 8, 12, 18)
        for n, (a, b) in enumerate(zip(cuts, cuts[1:])):
            ready = phase * tiles + (tiles if turned else -(-b // TILE))
            pieces.append(
                dict(
                    phase=phase,
                    store=store_of,
                    columns=(a, b - a),
                    x_first=n % 2 == 0,
                    steps=[ready + gap for gap in gaps],
                    take=takes.get(phase) if a == 0 else None,
                    give=gives.get(phase) if b == columns else None,
                )
            )
    shape = lambda *s: pltpu.VMEM(s, BF)

    def store(rows, columns):
        return [
            shape(8 * rows, columns),
            shape(4, rows, columns),
            shape(2, rows, columns),
            shape(2, rows, columns),
            *[shape(rows, columns)] * 4,
        ]

    any_ = pl.BlockSpec(memory_space=pl.ANY)
    vmem = pl.BlockSpec(memory_space=pltpu.VMEM)
    blocks = [jax.ShapeDtypeStruct((f // 8, d) if turned else (d // 8, f), BF) for _, turned, _, _ in phases]
    return pl.pallas_call(
        functools.partial(gradients_kernel, phases, pieces, tiles),
        out_shape=blocks + [jax.ShapeDtypeStruct((8, LANES), F32)],
        in_specs=[any_] * 10,
        out_specs=[vmem] * 7,
        scratch_shapes=[
            pltpu.VMEM((2, d, tokens), BF),
            pltpu.VMEM((2, tokens, TILE), BF),
            pltpu.SemaphoreType.DMA((2,)),
            pltpu.SemaphoreType.DMA((2,)),
            *store(d // 8, f),
            *store(d // 8, f),
            *store(f // 8, d),
            pltpu.VMEM((8, LANES), F32),
            pltpu.VMEM((8, 8, LANES), F32),
            pltpu.SemaphoreType.DMA((len(pieces), Sum.COPIES)),
            pltpu.SemaphoreType.DMA((len(pieces), Sum.COPIES)),
            pltpu.SemaphoreType.DMA((7,)),
            pltpu.SemaphoreType.DMA((7,)),
            pltpu.SemaphoreType.REGULAR((3, 4)),
        ],
        compiler_params=pltpu.CompilerParams(collective_id=2, has_side_effects=True, vmem_limit_bytes=67_043_328),
        cost_estimate=pl.CostEstimate(flops=12 * tokens * d * f, bytes_accessed=150_000_000, transcendentals=0),
        name="gradients",
    )(*lefts, *rights)


def adamw(w, m, v, g):
    m = 0.9 * m + 0.1 * g
    v = 0.95 * v + 0.05 * g * g
    step = m * lax.rsqrt(v + 1e-8) + 0.1 * w
    return (w - 0.02 * step).astype(jnp.bfloat16), m, v


def solution(mesh):
    def step(x, dy, *arrays):
        weights, m, v = (arrays[i : i + 3] for i in (0, 3, 6))
        wg, wu, wd = weights
        x, dy = x[0], dy[0]
        g, u, hid0, at0, wd0, wg1, wu1 = gate_up(x, wg, wu, wd)
        h, wd1 = down(hid0, x, wd0, wd)
        hid1, dg1, du1, at1, dyt, dh, dht = last_layer(h, dy, wg1, wu1, wd1)
        dg0, du0 = back_to_hidden(dh, g, u, wd0)
        d1, g1, u1, d0, g0, u0, squares = gradients((dyt, at1, dht, at0), (hid1, dg1, du1, hid0, dg0, du0))
        own = [jnp.stack(pair).astype(F32) for pair in ((g0, g1), (u0, u1), (d0, d1))]
        count = lax.psum(1, "s") * sum(g.size for g in own)
        factor = jnp.minimum(1.0, 0.5 * lax.rsqrt(jnp.sum(squares) / count + 1e-30))
        new = [adamw(w.astype(F32), m, v, g * factor) for w, m, v, g in zip(weights, m, v, own, strict=True)]
        return tuple(one[which] for which in range(3) for one in new)

    states, cut = P(("rep", "r", "s"), None, None), P(None, "s", None)
    return jax.shard_map(
        step,
        mesh=mesh,
        in_specs=(states, states) + (cut,) * 9,
        out_specs=(P("rep", "s", None),) * 9,
        check_vma=False,
    )
```

profile of v0, /device:TPU:0, one launch (start us, length us, event | category | flops | bytes accessed | tf_op | source)
XLA Modules:
  0.0 517.3 jit_solution(2279623451292309965)
XLA Ops:
  0.6 115.0 %gate_up.1 = (f32[4096,2304]{1,0:T(8,128)}, f32[4096,2304]{1,0:T(8,128)}, bf16[4096,2304]{1,0:T(8,128)(2,1)}, bf16[896,4096]{1,0:T(8,128)(2,1)}, bf16[2304,896]{...) custom-call(bf16[4096,896]{1,0:T(8,128)(2,1)} %bitcast.14, bf16[2,112,2304]{2,1,0:T(8,128)(2,1)} %wg_ref.1, ...), custom_call_target="tpu_custom_call" | custom-call | flops 33822867456 | bytes 110000000 | tf_op jit(solution)/shard_map/gate_up/pallas_call | solution.py:217
  115.7 32.4 %down.1 = (bf16[4096,896]{1,0:T(8,128)(2,1)}, bf16[2304,896]{1,0:T(8,128)(2,1)}) custom-call(bf16[4096,2304]{1,0:T(8,128)(2,1)} %get-tuple-element.34.hid_ref.refs_7_, bf16[4096,896]{1,0:T(8,128)(2,1)} %bitcast.15, bf16[2304,896]{1,0:T(8,128)(2,1)} %get-tuple-element.35.w_ref.wd_ref, bf16[2,288,896]{2,1,0:T(8,128)(2,1)} %wd_ref.3), custom_call_target="tpu_custom_call" | custom-call | flops 16911433728 | bytes 37000000 | tf_op jit(solution)/shard_map/down/pallas_call | solution.py:259
  148.1 123.3 %last_layer.1 = (bf16[4096,2304]{1,0:T(8,128)(2,1)}, bf16[4096,2304]{1,0:T(8,128)(2,1)}, bf16[4096,2304]{1,0:T(8,128)(2,1)}, bf16[896,4096]{1,0:T(8,128)(2,1)}, ...) custom-call(bf16[4096,896]{1,0:T(8,128)(2,1)} %get-tuple-element.36.h_ref, ...), custom_call_target="tpu_custom_call" | custom-call | flops 84557168640 | bytes 110000000 | tf_op jit(solution)/shard_map/last_layer/pallas_call | solution.py:315
  271.4 50.4 %back_to_hidden.1 = (bf16[4096,2304]{1,0:T(8,128)(2,1)}, bf16[4096,2304]{1,0:T(8,128)(2,1)}) custom-call(bf16[4096,896]{1,0:T(8,128)(2,1)} %get-tuple-element.47.dh_ref, f32[4096,2304]{1,0:T(8,128)} %get-tuple-element.48.g_ref, f32[4096,2304]{1,0:T(8,128)} %get-tuple-element.49.u_ref, bf16[2304,896]{1,0:T(8,128)(2,1)} %get-tuple-element.35.w_ref.wd_ref), custom_call_target="tpu_custom_call" | custom-call | flops 16911433728 | bytes 125000000 | tf_op jit(solution)/shard_map/back_to_hidden/pallas_call | solution.py:343
  321.8 181.0 %gradients.1 = (bf16[288,896]{1,0:T(8,128)(2,1)}, bf16[112,2304]{1,0:T(8,128)(2,1)}, bf16[112,2304]{1,0:T(8,128)(2,1)}, bf16[288,896]{1,0:T(8,128)(2,1)}, bf16[1...) custom-call(bf16[896,4096]{1,0:T(8,128)(2,1)} %get-tuple-element.40.refs_0_, ...), custom_call_target="tpu_custom_call" | custom-call | flops 101468602368 | bytes 150000000 | tf_op jit(solution)/shard_map/gradients/pallas_call | solution.py:611
  502.8 1.3 reduce_sum.9
  504.8 0.0 copy-start
  504.8 0.0 copy-start.1
  504.8 0.0 copy-start.2
  504.8 0.0 copy-start.3
  504.8 0.0 copy-start.4
  504.8 9.0 %fusion.2 = (bf16[2,112,2304]{2,1,0:T(8,128)(2,1)}, f32[2,112,2304]{2,1,0:T(8,128)}, f32[2,112,2304]{2,1,0:T(8,128)}, bf16[2,112,2304]{2,1,0:T(8,128)(2,1)}, f32...) fusion(bf16[2,112,2304]{2,1,0:T(8,128)(2,1)} %wg_ref.1, f32[]{:T(128)S(6)} %min_shard_map.3, ...), kind=kLoop, calls=%fused_computation.11 | loop fusion | flops 20643840 | bytes 22708228 | tf_op jit(solution)/shard_map/convert_element_type | solution.py:642
  513.8 0.0 copy-done
  513.8 0.0 copy-done.1
  513.9 0.0 copy-done.2
  513.9 0.0 copy-done.3
  513.9 0.4 copy-done.4
  514.3 3.0 fusion.8
Async XLA Ops:
  504.8 9.0 %copy-start = (f32[2,288,896]{2,1,0:T(8,128)S(1)}, f32[2,288,896]{2,1,0:T(8,128)}, u32[]{:S(2)}) copy-start(f32[2,288,896]{2,1,0:T(8,128)} %param.21) | copy-start | bytes 6193156
  504.8 9.0 %copy-start.1 = (f32[2,288,896]{2,1,0:T(8,128)S(1)}, f32[2,288,896]{2,1,0:T(8,128)}, u32[]{:S(2)}) copy-start(f32[2,288,896]{2,1,0:T(8,128)} %param.18) | copy-start | bytes 6193156
  504.8 9.0 %copy-start.2 = (bf16[2,288,896]{2,1,0:T(8,128)(2,1)S(1)}, bf16[2,288,896]{2,1,0:T(8,128)(2,1)}, u32[]{:S(2)}) copy-start(bf16[2,288,896]{2,1,0:T(8,128)(2,1)} %wd_ref.3) | copy-start | bytes 3096580
  504.8 9.0 %copy-start.3 = (bf16[288,896]{1,0:T(8,128)(2,1)S(1)}, bf16[288,896]{1,0:T(8,128)(2,1)}, u32[]{:S(2)}) copy-start(bf16[288,896]{1,0:T(8,128)(2,1)} %get-tuple-element.58) | copy-start | bytes 1548292
  504.8 9.5 %copy-start.4 = (bf16[288,896]{1,0:T(8,128)(2,1)S(1)}, bf16[288,896]{1,0:T(8,128)(2,1)}, u32[]{:S(2)}) copy-start(bf16[288,896]{1,0:T(8,128)(2,1)} %get-tuple-element.57) | copy-start | bytes 1548292
where the time goes:
time: 517 us
  Pallas kernels  502 us (97%)
  other arithmetic  13.2 us (3%)
    pallas_call x1, Pallas kernels, gradients(): pl.pallas_call(functools.partial(gradients_kernel, phases, pieces, tiles)...  181 us
    pallas_call x1, Pallas kernels, last_layer(): pl.pallas_call(last_kernel, grid=(tokens // tile,), out_shape=[shape(toke...  123 us
    pallas_call x1, Pallas kernels, gate_up(): pl.pallas_call(functools.partial(gate_up_kernel, parts, tiles), grid=(par...  115 us
    pallas_call x1, Pallas kernels, back_to_hidden(): pl.pallas_call(back_kernel, grid=(tokens // tile,), out_shape=[jax.ShapeD...  50.4 us
    pallas_call x1, Pallas kernels, down(): pl.pallas_call(functools.partial(down_kernel, tokens // tile), grid=(toke...  32.4 us
    convert_element_type x2, other arithmetic, adamw(): return ((w - 0.02 * step).astype(jnp.bfloat16), m, v)  12 us

commit v1 on v0

--- a/solution.py
+++ b/solution.py
@@ -35,86 +35,73 @@
         self.other, self.xn, self.yn, self.diagonal = at(x, y, 1 - core), at(1 - x, y, core), at(x, 1 - y, core), at(1 - x, 1 - y, core)
 
     def neighbours(self):
-        return ({"s": self.other}, {"s": self.xn}, {"s": self.yn}, {"r": 1 - self.z})
+        return ({"s": self.other}, {"s": self.xn}, {"s": self.yn}, {"r": 1 - self.z}, {"s": self.diagonal})
 
     def barrier(self):
         barrier = pltpu.get_barrier_semaphore()
         for device in self.neighbours():
             pl.semaphore_signal(barrier, inc=1, device_id=device, device_id_type=MESH)
-        pl.semaphore_wait(barrier, 4)
+        pl.semaphore_wait(barrier, len(self.neighbours()))
 
 
 TRANSFERS = 13
 
 
 class Gather:
-    def __init__(self, place, block, whole, split, sems):
-        self.p, self.block, self.whole = place, block, whole
+    def __init__(self, place, block, whole, axis, sems):
+        self.p, self.block, self.whole, self.axis = place, block, whole, axis
         self.rows = block.shape[0]
-        self.axis, first, second = split
-        self.parts = ((0, first), (first, second))
-        self.half = first + second
+        size = block.shape[axis]
+        grain = LANES if axis else 16
+        self.half = size // 2
+        self.first = (self.half // grain + 1) // 2 * grain
         self.send, self.recv, self.local = sems
-
-    def at(self, s):
-        return self.whole.at[pl.ds(pl.multiple_of(s * self.rows, 16), self.rows)]
-
-    def part(self, s, z, which):
-        start, size = self.parts[which]
-        offset = z * self.half + start
-        if self.axis == 1:
-            return self.at(s).at[:, pl.ds(pl.multiple_of(offset, LANES), size)]
-        return self.whole.at[pl.ds(pl.multiple_of(s * self.rows + offset, 16), size)]
+        core, xn, yn, zn, diagonal = place.neighbours()
+        z, inner = place.z, size - self.first
+        most, half = (z * self.first, inner), (z * self.half, self.half)
+        edge, edge2 = (z * inner, self.first), ((1 - z) * inner, self.first)
+        own, x, y, d = place.s, place.xn, place.yn, place.diagonal
+        half2 = ((1 - z) * self.half, self.half)
+        every = [(own, (0, size), core), (own, most, xn), (own, most, yn), (own, half, diagonal)]
+        every += [(x, most, core), (y, most, core), (d, half, core), (x, edge, zn), (y, edge, zn), (d, half, zn)]
+        every += [(x, edge2, core), (y, edge2, core), (d, half2, core)]
+        self.every = every
+
+    def part(self, ref, s, offset, size):
+        start = 0 if s is None else pl.multiple_of(s * self.rows, 16)
+        if self.axis:
+            return ref.at[pl.ds(start, self.rows), pl.ds(pl.multiple_of(offset, LANES), size)]
+        return ref.at[pl.ds(start + pl.multiple_of(offset, 16), size)]
 
     def copy(self, k):
-        p, z = self.p, self.p.z
-        core, xn, yn, zn = self.p.neighbours()
-        source, target, device = {
-            0: lambda: (self.block, self.at(p.s), core),
-            1: lambda: (self.block, self.at(p.s), xn),
-            2: lambda: (self.block, self.at(p.s), yn),
-            3: lambda: (self.at(p.xn), self.at(p.xn), core),
-            4: lambda: (self.at(p.yn), self.at(p.yn), core),
-            5: lambda: (self.part(p.xn, z, 0), self.part(p.xn, z, 0), yn),
-            6: lambda: (self.part(p.yn, z, 1), self.part(p.yn, z, 1), xn),
-            7: lambda: (self.part(p.diagonal, z, 0), self.part(p.diagonal, z, 0), zn),
-            8: lambda: (self.part(p.diagonal, z, 1), self.part(p.diagonal, z, 1), zn),
-            9: lambda: (self.part(p.diagonal, z, 0), self.part(p.diagonal, z, 0), core),
-            10: lambda: (self.part(p.diagonal, z, 1), self.part(p.diagonal, z, 1), core),
-            11: lambda: (self.part(p.diagonal, 1 - z, 0), self.part(p.diagonal, 1 - z, 0), core),
-            12: lambda: (self.part(p.diagonal, 1 - z, 1), self.part(p.diagonal, 1 - z, 1), core),
-        }[k]()
+        s, (offset, size), device = self.every[k]
+        target = self.part(self.whole, s, offset, size)
+        source = self.part(self.block, None, offset, size) if s is self.p.s else target
         return pltpu.make_async_remote_copy(
             src_ref=source, dst_ref=target, send_sem=self.send.at[k], recv_sem=self.recv.at[k], device_id=device, device_id_type=MESH
         )
 
     def keep(self):
-        return pltpu.make_async_copy(self.block, self.at(self.p.s), self.local)
+        return pltpu.make_async_copy(self.block, self.whole.at[pl.ds(pl.multiple_of(self.p.s * self.rows, 16), self.rows)], self.local)
 
     def start(self):
-        for k in (1, 2, 0):
+        for k in (1, 2, 3, 0):
             self.copy(k).start()
         self.keep().start()
 
-    def passing(self, after, then):
-        self.copy(after).wait_recv()
-        for k in then:
+    def second(self):
+        for k in (1, 2, 3):
+            self.copy(k).wait_recv()
+        for k in (7, 8, 9, 4, 5, 6):
             self.copy(k).start()
 
-    def second(self):
-        self.passing(1, (5, 3))
-        self.passing(2, (6, 4))
-
     def third(self):
-        self.passing(5, (7, 9))
-        self.passing(6, (8, 10))
-
-    def fourth(self):
-        self.passing(7, (11,))
-        self.passing(8, (12,))
+        for k in (7, 8, 9):
+            self.copy(k).wait_recv()
+            self.copy(k + 3).start()
 
     def finish(self):
-        for k in (0, 3, 4, 9, 10, 11, 12):
+        for k in (0, 4, 5, 6, 10, 11, 12):
             self.copy(k).wait_recv()
         for k in range(TRANSFERS):
             self.copy(k).wait_send()
@@ -123,12 +110,6 @@
 
 def gather_sems(jobs):
     return [pltpu.SemaphoreType.DMA((jobs, TRANSFERS)), pltpu.SemaphoreType.DMA((jobs, TRANSFERS)), pltpu.SemaphoreType.DMA((jobs,))]
-
-
-def halves_of(columns):
-    half = columns // 2
-    first = (half // LANES + 1) // 2 * LANES
-    return first, half - first
 
 
 def on(step, *actions):
@@ -147,47 +128,30 @@
     step = part * tiles + tile
     place = Place()
     width = g_ref.shape[1]
-    sems = lambda j: (send.at[j], recv.at[j], local.at[j])
-    jobs = []
-    for n in range(parts):
-        cols = pl.ds(n * width, width)
-        for i, (own, whole) in enumerate(((wg_ref, wg), (wu_ref, wu))):
-            jobs.append(Gather(place, own.at[0, :, cols], whole.at[:, cols], (1, *halves_of(width)), sems(2 * n + i)))
-    rows = wd_ref.shape[1]
-    down = Gather(place, wd_ref.at[0], wd0_ref, (0, (rows // 2 // 16 + 1) // 2 * 16, rows // 2 - (rows // 2 // 16 + 1) // 2 * 16), sems(2 * parts))
-    gate1 = Gather(place, wg_ref.at[1], wg1_ref, (1, *halves_of(wg_ref.shape[2])), sems(2 * parts + 1))
-    up1 = Gather(place, wu_ref.at[1], wu1_ref, (1, *halves_of(wu_ref.shape[2])), sems(2 * parts + 2))
-    b = lambda n, what: [getattr(jobs[2 * n + i], what) for i in range(2)]
+    f = wg_ref.shape[2]
+    middle = (f // LANES + 2) // 4 * 2 * LANES
+    ranges = [(own.at[0], whole, pl.ds(n * width, width), 1) for n in range(parts) for own, whole in ((wg_ref, wg), (wu_ref, wu))]
+    ranges += [(wd_ref.at[0], wd0_ref, pl.ds(0, wd_ref.shape[2]), 0), (wg_ref.at[1], wg1_ref, pl.ds(0, f), 1)]
+    ranges += [(wu_ref.at[1], wu1_ref, cols, 1) for cols in (pl.ds(0, middle), pl.ds(middle, f - middle))]
+    jobs = [
+        Gather(place, own.at[:, cols], whole.at[:, cols], axis, (send.at[k], recv.at[k], local.at[k])) for k, (own, whole, cols, axis) in enumerate(ranges)
+    ]
+    b0, b1, b2, (down, gate1), up1 = [jobs[k : k + 2] for k in range(0, len(jobs), 2)]
+    both = lambda pair, *stages: [getattr(job, stage) for stage in stages for job in pair]
     last = parts * tiles - 1
 
-    on(
-        step == 0,
-        place.barrier,
-        *b(0, "start"),
-        *b(0, "second"),
-        *b(1, "start"),
-        *b(0, "third"),
-        *b(0, "fourth"),
-        *b(0, "finish"),
-        *b(1, "second"),
-        *b(2, "start"),
-    )
-    on(step == 2, *b(1, "third"))
-    on(step == 3, *b(1, "fourth"))
-    on(step == 4, down.start)
-    on(step == 5, *b(2, "second"))
-    on(step == 7, *b(2, "third"))
-    on(step == 8, *b(1, "finish"))
-    on(step == 9, *b(2, "fourth"), gate1.start)
-    on(step == 11, down.second)
-    on(step == 13, down.third)
-    on(step == 14, up1.start)
-    on(step == 15, down.fourth)
-    on(step == 16, *b(2, "finish"))
-    on(step == 17, gate1.second, down.finish)
-    on(step == 19, gate1.third)
-    on(step == 21, gate1.fourth)
-    on(step == 22, up1.second, gate1.finish)
+    on(step == 0, place.barrier, *both(b0, "start"), *both(b1, "start"), *both(b0, "second", "third", "finish"), *both(b2, "start"))
+    on(step == 1, *both(b1, "second"), down.start)
+    on(step == 5, *both(b2, "second"), gate1.start)
+    on(step == 6, *both(b1, "third"))
+    on(step == tiles, *both(b1, "finish"))
+    on(step == 10, *both(b2, "third"), down.second)
+    on(step == 11, *both(up1, "start"))
+    on(step == 2 * tiles, *both(b2, "finish"), down.third, gate1.second)
+    on(step == 18, down.finish)
+    on(step == 20, up1[0].second)
+    on(step == 22, gate1.third)
+    on(step == last, gate1.finish, up1[1].second)
 
     h = wide(h_ref[...])
     a = (h * scale_of(h)).astype(BF)
@@ -204,7 +168,7 @@
         u_ref[:, n : n + 256] = u
         hid_ref[:, n : n + 256] = (g * sigmoid(g) * u).astype(BF)
 
-    on(step == last, up1.third, up1.fourth, up1.finish)
+    on(step == last, *both(up1, "third", "finish"))
 
 
 def gate_up(h, wg, wu, wd):
@@ -229,7 +193,7 @@
         in_specs=[pl.BlockSpec((tile, d), lambda p, t: (t, 0)), any_, any_, any_],
         out_specs=[pl.BlockSpec((tile, width), lambda p, t: (t, p))] * 3
         + [pl.BlockSpec((d, tile), lambda p, t: (0, jnp.where(p == 0, t, tiles - 1))), any_, any_, any_],
-        scratch_shapes=[pltpu.VMEM((d, f), BF)] * 2 + gather_sems(2 * parts + 3),
+        scratch_shapes=[pltpu.VMEM((d, f), BF)] * 2 + gather_sems(2 * parts + 4),
         compiler_params=pltpu.CompilerParams(
             collective_id=0, has_side_effects=True, vmem_limit_bytes=LIMIT, dimension_semantics=("arbitrary", "arbitrary")
         ),
@@ -241,14 +205,17 @@
 def down_kernel(tiles, hid_ref, h_ref, w_ref, wd_ref, h1_ref, wd1_ref, send, recv, local):
     step = pl.program_id(0)
     place = Place()
-    sems = lambda j: (send.at[j], recv.at[j], local.at[j])
-    rows = wd_ref.shape[1]
-    down = Gather(place, wd_ref.at[1], wd1_ref, (0, (rows // 2 // 16 + 1) // 2 * 16, rows // 2 - (rows // 2 // 16 + 1) // 2 * 16), sems(0))
-    on(step == 0, place.barrier, down.start)
-    on(step == tiles // 2 + 1, down.second)
-    on(step == tiles // 2 + 2, down.third)
+    d = wd_ref.shape[2]
+    middle = (d // LANES + 1) // 2 * LANES
+    jobs = [
+        Gather(place, wd_ref.at[1, :, cols], wd1_ref.at[:, cols], 0, (send.at[k], recv.at[k], local.at[k]))
+        for k, cols in enumerate((pl.ds(0, middle), pl.ds(middle, d - middle)))
+    ]
+    on(step == 0, place.barrier, *[job.start for job in jobs])
+    on(step == tiles - 3, jobs[0].second)
+    on(step == tiles - 1, jobs[1].second)
     h1_ref[...] = h_ref[...] + dot(hid_ref[...], w_ref[...]).astype(BF)
-    on(step == tiles - 1, down.fourth, down.finish)
+    on(step == tiles - 1, *[job.third for job in jobs], *[job.finish for job in jobs])
 
 
 def down(hid, h, w, wd):
@@ -267,7 +234,7 @@
             any_,
         ],
         out_specs=[pl.BlockSpec((tile, d), lambda t: (t, 0)), any_],
-        scratch_shapes=gather_sems(1),
+        scratch_shapes=gather_sems(2),
         compiler_params=pltpu.CompilerParams(collective_id=1, has_side_effects=True, vmem_limit_bytes=LIMIT, dimension_semantics=("arbitrary",)),
         cost_estimate=pl.CostEstimate(flops=2 * tokens * d * f, bytes_accessed=37_000_000, transcendentals=0),
         name="down",
@@ -372,7 +339,7 @@
         return pl.ds(pl.multiple_of((chip * 2 + core) * self.rows, 16), self.rows)
 
     def copy(self, k):
-        core, xn, yn, zn = self.p.neighbours()
+        core, xn, yn, zn, _ = self.p.neighbours()
         first, second = (xn, yn) if self.x_first else (yn, xn)
         if k < 4:
             source, target, device = self.term.at[self.block(k, 1 - self.core), self.cols], self.rc.at[k, :, self.cols], core
@@ -473,7 +440,7 @@
     pl.semaphore_wait(barrier, 8)
 
     sums = [Sum(place, stores[p["store"]], outs[p["phase"]], squares, p["columns"], p["x_first"], send.at[q], recv.at[q]) for q, p in enumerate(pieces)]
-    neighbours = place.neighbours()
+    neighbours = place.neighbours()[:4]
 
     def give(pair):
         for d, device in enumerate(neighbours):
@@ -579,8 +546,8 @@
     for phase, (_, turned, store_of, _) in enumerate(phases):
         final = phase == len(phases) - 1
         columns = d if turned else f
-        cuts = [0, 3 * TILE, 6 * TILE, columns - 3 * LANES, columns] if final else [0, -(-columns // 2 // LANES) * LANES, columns]
-        gaps = (0, 2, 6, 9, 12) if final else (0, 2, 8, 12, 18)
+        cuts = [0, 3 * TILE, 6 * TILE, columns - TILE, columns] if final else [0, -(-columns // 2 // LANES) * LANES, columns]
+        gaps = (0, 3, 10, 16, 21) if final else (0, 3, 9, 15, 20)
         for n, (a, b) in enumerate(zip(cuts, cuts[1:])):
             ready = phase * tiles + (tiles if turned else -(-b // TILE))
             pieces.append(

time: 517 us -> 488 us (0.944)
  Pallas kernels: 502 us -> 473 us
    pallas_call x1, Pallas kernels: 115 us -> 95.1 us  [gate_up(): pl.pallas_call(functools.partial(gate_up_kernel, parts, tiles), grid=(par...]
    pallas_call x1, Pallas kernels: 181 us -> 169 us  [gradients(): pl.pallas_call(functools.partial(gradients_kernel, phases, pieces, tiles)...]
where the time goes in v1:
time: 488 us
  Pallas kernels  473 us (97%)
  other arithmetic  13.2 us (3%)
    pallas_call x1, Pallas kernels, gradients(): pl.pallas_call(functools.partial(gradients_kernel, phases, pieces, tiles)...  169 us
    pallas_call x1, Pallas kernels, last_layer(): pl.pallas_call(last_kernel, grid=(tokens // tile,), out_shape=[shape(toke...  123 us
    pallas_call x1, Pallas kernels, gate_up(): pl.pallas_call(functools.partial(gate_up_kernel, parts, tiles), grid=(par...  95.1 us
    pallas_call x1, Pallas kernels, back_to_hidden(): pl.pallas_call(back_kernel, grid=(tokens // tile,), out_shape=[jax.ShapeD...  50.4 us
    pallas_call x1, Pallas kernels, down(): pl.pallas_call(functools.partial(down_kernel, tokens // tile), grid=(toke...  34.5 us
    convert_element_type x2, other arithmetic, adamw(): return ((w - 0.02 * step).astype(jnp.bfloat16), m, v)  12 us

profile of v1, /device:TPU:0, one launch (start us, length us, event | category | flops | bytes accessed | tf_op | source)
XLA Modules:
  0.0 487.8 jit_solution(8326439596641871656)
XLA Ops:
  0.6 95.1 %gate_up.1 = (f32[4096,2304]{1,0:T(8,128)}, f32[4096,2304]{1,0:T(8,128)}, bf16[4096,2304]{1,0:T(8,128)(2,1)}, bf16[896,4096]{1,0:T(8,128)(2,1)}, bf16[2304,896]{...) custom-call(bf16[4096,896]{1,0:T(8,128)(2,1)} %bitcast.14, bf16[2,112,2304]{2,1,0:T(8,128)(2,1)} %wg_ref.1, ...), custom_call_target="tpu_custom_call" | custom-call | flops 33822867456 | bytes 110000000 | tf_op jit(solution)/shard_map/gate_up/pallas_call | solution.py:181
  95.8 34.5 %down.1 = (bf16[4096,896]{1,0:T(8,128)(2,1)}, bf16[2304,896]{1,0:T(8,128)(2,1)}) custom-call(bf16[4096,2304]{1,0:T(8,128)(2,1)} %get-tuple-element.34.hid_ref.refs_7_, bf16[4096,896]{1,0:T(8,128)(2,1)} %bitcast.15, bf16[2304,896]{1,0:T(8,128)(2,1)} %get-tuple-element.35.w_ref.wd_ref, bf16[2,288,896]{2,1,0:T(8,128)(2,1)} %wd_ref.3), custom_call_target="tpu_custom_call" | custom-call | flops 16911433728 | bytes 37000000 | tf_op jit(solution)/shard_map/down/pallas_call | solution.py:226
  130.3 123.3 %last_layer.1 = (bf16[4096,2304]{1,0:T(8,128)(2,1)}, bf16[4096,2304]{1,0:T(8,128)(2,1)}, bf16[4096,2304]{1,0:T(8,128)(2,1)}, bf16[896,4096]{1,0:T(8,128)(2,1)}, ...) custom-call(bf16[4096,896]{1,0:T(8,128)(2,1)} %get-tuple-element.36.h_ref, ...), custom_call_target="tpu_custom_call" | custom-call | flops 84557168640 | bytes 110000000 | tf_op jit(solution)/shard_map/last_layer/pallas_call | solution.py:282
  253.6 50.4 %back_to_hidden.1 = (bf16[4096,2304]{1,0:T(8,128)(2,1)}, bf16[4096,2304]{1,0:T(8,128)(2,1)}) custom-call(bf16[4096,896]{1,0:T(8,128)(2,1)} %get-tuple-element.47.dh_ref, f32[4096,2304]{1,0:T(8,128)} %get-tuple-element.48.g_ref, f32[4096,2304]{1,0:T(8,128)} %get-tuple-element.49.u_ref, bf16[2304,896]{1,0:T(8,128)(2,1)} %get-tuple-element.35.w_ref.wd_ref), custom_call_target="tpu_custom_call" | custom-call | flops 16911433728 | bytes 125000000 | tf_op jit(solution)/shard_map/back_to_hidden/pallas_call | solution.py:310
  304.0 169.4 %gradients.1 = (bf16[288,896]{1,0:T(8,128)(2,1)}, bf16[112,2304]{1,0:T(8,128)(2,1)}, bf16[112,2304]{1,0:T(8,128)(2,1)}, bf16[288,896]{1,0:T(8,128)(2,1)}, bf16[1...) custom-call(bf16[896,4096]{1,0:T(8,128)(2,1)} %get-tuple-element.40.refs_0_, ...), custom_call_target="tpu_custom_call" | custom-call | flops 101468602368 | bytes 150000000 | tf_op jit(solution)/shard_map/gradients/pallas_call | solution.py:578
  473.4 1.3 reduce_sum.9
  475.3 0.0 copy-start
  475.4 0.0 copy-start.1
  475.4 0.0 copy-start.2
  475.4 0.0 copy-start.3
  475.4 0.0 copy-start.4
  475.4 9.0 %fusion.2 = (bf16[2,112,2304]{2,1,0:T(8,128)(2,1)}, f32[2,112,2304]{2,1,0:T(8,128)}, f32[2,112,2304]{2,1,0:T(8,128)}, bf16[2,112,2304]{2,1,0:T(8,128)(2,1)}, f32...) fusion(bf16[2,112,2304]{2,1,0:T(8,128)(2,1)} %wg_ref.1, f32[]{:T(128)S(6)} %min_shard_map.3, ...), kind=kLoop, calls=%fused_computation.11 | loop fusion | flops 20643840 | bytes 22708228 | tf_op jit(solution)/shard_map/convert_element_type | solution.py:609
  484.4 0.0 copy-done
  484.4 0.0 copy-done.1
  484.4 0.0 copy-done.2
  484.4 0.0 copy-done.3
  484.4 0.4 copy-done.4
  484.9 3.0 fusion.8
Async XLA Ops:
  475.3 9.0 %copy-start = (f32[2,288,896]{2,1,0:T(8,128)S(1)}, f32[2,288,896]{2,1,0:T(8,128)}, u32[]{:S(2)}) copy-start(f32[2,288,896]{2,1,0:T(8,128)} %param.21) | copy-start | bytes 6193156
  475.4 9.0 %copy-start.1 = (f32[2,288,896]{2,1,0:T(8,128)S(1)}, f32[2,288,896]{2,1,0:T(8,128)}, u32[]{:S(2)}) copy-start(f32[2,288,896]{2,1,0:T(8,128)} %param.18) | copy-start | bytes 6193156
  475.4 9.0 %copy-start.2 = (bf16[2,288,896]{2,1,0:T(8,128)(2,1)S(1)}, bf16[2,288,896]{2,1,0:T(8,128)(2,1)}, u32[]{:S(2)}) copy-start(bf16[2,288,896]{2,1,0:T(8,128)(2,1)} %wd_ref.3) | copy-start | bytes 3096580
  475.4 9.0 %copy-start.3 = (bf16[288,896]{1,0:T(8,128)(2,1)S(1)}, bf16[288,896]{1,0:T(8,128)(2,1)}, u32[]{:S(2)}) copy-start(bf16[288,896]{1,0:T(8,128)(2,1)} %get-tuple-element.58) | copy-start | bytes 1548292
  475.4 9.5 %copy-start.4 = (bf16[288,896]{1,0:T(8,128)(2,1)S(1)}, bf16[288,896]{1,0:T(8,128)(2,1)}, u32[]{:S(2)}) copy-start(bf16[288,896]{1,0:T(8,128)(2,1)} %get-tuple-element.57) | copy-start | bytes 1548292

commit v2 on v1

--- a/solution.py
+++ b/solution.py
@@ -241,28 +241,37 @@
     )(hid, h, w, wd)
 
 
-def last_kernel(h_ref, dy_ref, wg_ref, wu_ref, wd_ref, hid_ref, dg_ref, du_ref, at_ref, dyt_ref, dh_ref, dht_ref):
+def last_kernel(h_ref, dy_ref, wg_ref, wu_ref, wd_ref, hid_ref, dg_ref, du_ref, at_ref, dyt_ref, dh_ref, dht_ref, gt, ut, dt):
     h = wide(h_ref[...])
     scale = scale_of(h)
     a = (h * scale).astype(BF)
     dy = dy_ref[...]
+    f = wg_ref.shape[1]
+
+    @pl.when(pl.program_id(0) == 0)
+    def _():
+        for n in range(0, f, 256):
+            where = slice(n, n + 256)
+            gt[where, :] = wg_ref[:, where].T
+            ut[where, :] = wu_ref[:, where].T
+            dt[:, where] = wd_ref[where, :].T
+
     at_ref[...] = a.T
     dyt_ref[...] = dy.T
-    f = wg_ref.shape[1]
     by_a = jnp.zeros(h.shape, F32)
     for n in range(0, f, 768):
         for k in range(n, n + 768, 256):
             where = slice(k, k + 256)
             g = dot(a, wg_ref[:, where])
             u = dot(a, wu_ref[:, where])
-            back = wide(dot(dy, wd_ref[where, :], ((1,), (1,))).astype(BF))
+            back = wide(dot(dy, dt[:, where]).astype(BF))
             s = sigmoid(g)
             silu = g * s
             hid_ref[:, where] = (silu * u).astype(BF)
             du_ref[:, where] = (back * silu).astype(BF)
             dg_ref[:, where] = (back * u * (s * (1.0 + g * (1.0 - s)))).astype(BF)
         where = slice(n, n + 768)
-        by_a += dot(dg_ref[:, where], wg_ref[:, where], ((1,), (1,))) + dot(du_ref[:, where], wu_ref[:, where], ((1,), (1,)))
+        by_a += dot(dg_ref[:, where], gt[where, :]) + dot(du_ref[:, where], ut[where, :])
     by_a = wide(by_a.astype(BF))
     mean = jnp.mean(by_a * h, -1, keepdims=True)
     by_h = (by_a * scale - h * (scale * scale * scale * mean)).astype(BF)
@@ -285,38 +294,11 @@
         out_shape=[shape(tokens, f)] * 3 + [shape(d, tokens)] * 2 + [shape(tokens, d), shape(d, tokens)],
         in_specs=[rows(d), rows(d), fixed(d, f), fixed(d, f), fixed(f, d)],
         out_specs=[rows(f)] * 3 + [columns] * 2 + [rows(d), columns],
+        scratch_shapes=[pltpu.VMEM((f, d), BF)] * 2 + [pltpu.VMEM((d, f), BF)],
         compiler_params=pltpu.CompilerParams(vmem_limit_bytes=LIMIT, dimension_semantics=("arbitrary",)),
         cost_estimate=pl.CostEstimate(flops=10 * tokens * d * f, bytes_accessed=110_000_000, transcendentals=tokens * f),
         name="last_layer",
     )(h, dy, wg, wu, wd)
-
-
-def back_kernel(dh_ref, g_ref, u_ref, wd_ref, dg_ref, du_ref):
-    dh = dh_ref[...]
-    for k in range(0, g_ref.shape[1], 256):
-        where = slice(k, k + 256)
-        back = wide(dot(dh, wd_ref[where, :], ((1,), (1,))).astype(BF))
-        g, u = g_ref[:, where], u_ref[:, where]
-        s = sigmoid(g)
-        du_ref[:, where] = (back * (g * s)).astype(BF)
-        dg_ref[:, where] = (back * u * (s * (1.0 + g * (1.0 - s)))).astype(BF)
-
-
-def back_to_hidden(dh, g, u, wd):
-    tokens, d = dh.shape
-    f = g.shape[1]
-    tile = 512
-    rows = lambda n: pl.BlockSpec((tile, n), lambda t: (t, 0))
-    return pl.pallas_call(
-        back_kernel,
-        grid=(tokens // tile,),
-        out_shape=[jax.ShapeDtypeStruct((tokens, f), BF)] * 2,
-        in_specs=[rows(d), rows(f), rows(f), pl.BlockSpec((f, d), lambda t: (0, 0), pipeline_mode=pl.Buffered(1))],
-        out_specs=[rows(f)] * 2,
-        compiler_params=pltpu.CompilerParams(vmem_limit_bytes=LIMIT, dimension_semantics=("arbitrary",)),
-        cost_estimate=pl.CostEstimate(flops=2 * tokens * d * f, bytes_accessed=125_000_000, transcendentals=tokens * f),
-        name="back_to_hidden",
-    )(dh, g, u, wd)
 
 
 class Sum:
@@ -422,12 +404,21 @@
 
 
 TILE = 256
+CHUNK = 1024
+
+
+def split(items, *sizes):
+    parts = []
+    for size in sizes:
+        parts.append(items[:size])
+        items = items[size:]
+    return parts, items
 
 
 def gradients_kernel(phases, pieces, tiles, *refs):
-    lefts, rights = refs[:4], refs[4:10]
-    outs, total_ref = refs[10:16], refs[16]
-    left, right, l_sem, r_sem, *rest = refs[17:]
+    (lefts, rights, (dh, gate, up, down), outs, (total_ref, dg, du)), rest = split(refs, 4, 4, 4, len(phases), 3)
+    rights = (*rights, dg, du)
+    left, right, l_sem, r_sem, dh_vmem, w_vmem, in_vmem, out_vmem, dh_sem, w_sem, in_sem, out_sem, *rest = rest
     stores = [rest[8 * i : 8 * i + 8] for i in range(3)]
     squares, parts, send, recv, psend, precv, free = rest[24:]
     place = Place()
@@ -457,8 +448,33 @@
         cols = pl.ds(pl.multiple_of(i * TILE, TILE), TILE)
         return pltpu.make_async_copy(rights[phase].at[:, cols], right.at[slot], r_sem.at[slot])
 
+    chunks = dh.shape[0] // CHUNK
+
+    def load_dh(n):
+        return pltpu.make_async_copy(dh.at[pl.ds(n * CHUNK, CHUNK)], dh_vmem, dh_sem)
+
+    def chunk_at(n, i):
+        return pl.ds(n * CHUNK, CHUNK), pl.ds(pl.multiple_of(i * TILE, TILE), TILE)
+
+    def load_chunk(n, i, slot):
+        rows, cols = chunk_at(n, i)
+        pairs = [(gate.at[rows, cols], in_vmem.at[slot, 0]), (up.at[rows, cols], in_vmem.at[slot, 1])]
+        copies = [pltpu.make_async_copy(a, b, in_sem.at[slot, k]) for k, (a, b) in enumerate(pairs)]
+        return [*copies, pltpu.make_async_copy(down.at[cols], w_vmem.at[slot], w_sem.at[slot])]
+
+    def store_chunk(n, i, slot):
+        rows, cols = chunk_at(n, i)
+        return [pltpu.make_async_copy(out_vmem.at[slot, k], ref.at[rows, cols], out_sem.at[slot, k]) for k, ref in enumerate((dg, du))]
+
+    def do(copies, what):
+        for copy in copies:
+            getattr(copy, what)()
+
     squares[...] = jnp.zeros_like(squares)
+    load_dh(0).start()
     load_left(0).start()
+    do(load_chunk(0, 0, 0), "start")
+    do(load_chunk(0, 1, 1), "start")
     load_right(0, 0, 0).start()
     load_left(1).start()
     load_right(0, 1, 1).start()
@@ -482,6 +498,8 @@
         if loads is not None:
             load_left(loads).start()
         term = stores[store][0]
+        if n < chunks:
+            load_dh(n).wait()
 
         def tile(i, carry, n=n, which=which, turned=turned, term=term):
             for k in range(tiles):
@@ -489,6 +507,14 @@
                     on(i == k, *[functools.partial(run, q, stage) for q, stage in at[n * tiles + k]])
             slot = (n * tiles + i) % slots
             load_right(n, i, slot).wait()
+            if n < chunks:
+                do(load_chunk(n, i, slot), "wait")
+                on(n * tiles + i >= slots, lambda: do(store_chunk(n, i, slot), "wait"))
+                back = wide(dot(dh_vmem[...], w_vmem[slot], ((1,), (1,))).astype(BF))
+                g, u = in_vmem[slot, 0], in_vmem[slot, 1]
+                sg = sigmoid(g)
+                out_vmem[slot, 0] = (back * u * (sg * (1.0 + g * (1.0 - sg)))).astype(BF)
+                out_vmem[slot, 1] = (back * (g * sg)).astype(BF)
             total = dot(left[which % 2], right[slot])
             where = pl.ds(pl.multiple_of(i * TILE, TILE), TILE)
             if turned:
@@ -496,19 +522,31 @@
             else:
                 term[:, where] = total.astype(BF)
 
+            if n < chunks:
+                do(store_chunk(n, i, slot), "start")
+
             @pl.when(i + slots < tiles)
             def _():
                 load_right(n, i + slots, slot).start()
+                if n < chunks:
+                    do(load_chunk(n, i + slots, slot), "start")
 
             if n + 1 < len(phases):
 
                 @pl.when(i + slots >= tiles)
                 def _():
                     load_right(n + 1, i + slots - tiles, slot).start()
+                    if n + 1 < chunks:
+                        do(load_chunk(n + 1, i + slots - tiles, slot), "start")
 
             return carry
 
         lax.fori_loop(0, tiles, tile, 0)
+        if n + 1 < chunks:
+            load_dh(n + 1).start()
+        if n + 1 == chunks:
+            for i in range(tiles - slots, tiles):
+                do(store_chunk(n, i, (n * tiles + i) % slots), "wait")
 
     for step in sorted(at):
         if step >= len(phases) * tiles:
@@ -536,7 +574,7 @@
     total_ref[...] = total
 
 
-def gradients(lefts, rights):
+def gradients(lefts, rights, dh, gate, up, down):
     d, tokens = lefts[0].shape
     f = rights[0].shape[1]
     tiles = f // TILE
@@ -577,14 +615,22 @@
     blocks = [jax.ShapeDtypeStruct((f // 8, d) if turned else (d // 8, f), BF) for _, turned, _, _ in phases]
     return pl.pallas_call(
         functools.partial(gradients_kernel, phases, pieces, tiles),
-        out_shape=blocks + [jax.ShapeDtypeStruct((8, LANES), F32)],
-        in_specs=[any_] * 10,
-        out_specs=[vmem] * 7,
+        out_shape=blocks + [jax.ShapeDtypeStruct((8, LANES), F32)] + [jax.ShapeDtypeStruct((tokens, f), BF)] * 2,
+        in_specs=[any_] * 12,
+        out_specs=[vmem] * 7 + [any_] * 2,
         scratch_shapes=[
             pltpu.VMEM((2, d, tokens), BF),
             pltpu.VMEM((2, tokens, TILE), BF),
             pltpu.SemaphoreType.DMA((2,)),
             pltpu.SemaphoreType.DMA((2,)),
+            pltpu.VMEM((CHUNK, d), BF),
+            pltpu.VMEM((2, TILE, d), BF),
+            pltpu.VMEM((2, 2, CHUNK, TILE), F32),
+            pltpu.VMEM((2, 2, CHUNK, TILE), BF),
+            pltpu.SemaphoreType.DMA,
+            pltpu.SemaphoreType.DMA((2,)),
+            pltpu.SemaphoreType.DMA((2, 2)),
+            pltpu.SemaphoreType.DMA((2, 2)),
             *store(d // 8, f),
             *store(d // 8, f),
             *store(f // 8, d),
@@ -597,9 +643,9 @@
             pltpu.SemaphoreType.REGULAR((3, 4)),
         ],
         compiler_params=pltpu.CompilerParams(collective_id=2, has_side_effects=True, vmem_limit_bytes=67_043_328),
-        cost_estimate=pl.CostEstimate(flops=12 * tokens * d * f, bytes_accessed=150_000_000, transcendentals=0),
+        cost_estimate=pl.CostEstimate(flops=14 * tokens * d * f, bytes_accessed=270_000_000, transcendentals=tokens * f),
         name="gradients",
-    )(*lefts, *rights)
+    )(*lefts, *rights, dh, gate, up, down)
 
 
 def adamw(w, m, v, g):
@@ -617,8 +663,7 @@
         g, u, hid0, at0, wd0, wg1, wu1 = gate_up(x, wg, wu, wd)
         h, wd1 = down(hid0, x, wd0, wd)
         hid1, dg1, du1, at1, dyt, dh, dht = last_layer(h, dy, wg1, wu1, wd1)
-        dg0, du0 = back_to_hidden(dh, g, u, wd0)
-        d1, g1, u1, d0, g0, u0, squares = gradients((dyt, at1, dht, at0), (hid1, dg1, du1, hid0, dg0, du0))
+        d1, g1, u1, d0, g0, u0, squares, *_ = gradients((dyt, at1, dht, at0), (hid1, dg1, du1, hid0), dh, g, u, wd0)
         own = [jnp.stack(pair).astype(F32) for pair in ((g0, g1), (u0, u1), (d0, d1))]
         count = lax.psum(1, "s") * sum(g.size for g in own)
         factor = jnp.minimum(1.0, 0.5 * lax.rsqrt(jnp.sum(squares) / count + 1e-30))

time: 488 us -> 483 us (0.990)
  Pallas kernels: 473 us -> 461 us
    pallas_call x1 -> x0, Pallas kernels: 50.4 us -> none  [back_to_hidden(): pl.pallas_call(back_kernel, grid=(tokens // tile,), out_shape=[jax.ShapeD...]
    pallas_call x1, Pallas kernels: 169 us -> 204 us  [gradients(): pl.pallas_call(functools.partial(gradients_kernel, phases, pieces, tiles)...]
where the time goes in v2:
time: 483 us; the launch traced here: 478 us
  Pallas kernels  461 us (95%)
  other arithmetic  13.4 us (3%)
    pallas_call x1, Pallas kernels, gradients(): pl.pallas_call(functools.partial(gradients_kernel, phases, pieces, tiles)...  204 us
    pallas_call x1, Pallas kernels, last_layer(): pl.pallas_call(last_kernel, grid=(tokens // tile,), out_shape=[shape(toke...  128 us
    pallas_call x1, Pallas kernels, gate_up(): pl.pallas_call(functools.partial(gate_up_kernel, parts, tiles), grid=(par...  95.2 us
    pallas_call x1, Pallas kernels, down(): pl.pallas_call(functools.partial(down_kernel, tokens // tile), grid=(toke...  34.5 us
    convert_element_type x2, other arithmetic, adamw(): return ((w - 0.02 * step).astype(jnp.bfloat16), m, v)  12.2 us

profile of v2, /device:TPU:0, one launch (start us, length us, event | category | flops | bytes accessed | tf_op | source)
XLA Modules:
  0.0 478.4 jit_solution(10427998434615271723)
XLA Ops:
  0.6 95.2 %gate_up.1 = (f32[4096,2304]{1,0:T(8,128)}, f32[4096,2304]{1,0:T(8,128)}, bf16[4096,2304]{1,0:T(8,128)(2,1)}, bf16[896,4096]{1,0:T(8,128)(2,1)}, bf16[2304,896]{...) custom-call(bf16[4096,896]{1,0:T(8,128)(2,1)} %bitcast.14, bf16[2,112,2304]{2,1,0:T(8,128)(2,1)} %wg_ref.1, ...), custom_call_target="tpu_custom_call" | custom-call | flops 33822867456 | bytes 110000000 | tf_op jit(solution)/shard_map/gate_up/pallas_call | solution.py:181
  95.9 34.5 %down.1 = (bf16[4096,896]{1,0:T(8,128)(2,1)}, bf16[2304,896]{1,0:T(8,128)(2,1)}) custom-call(bf16[4096,2304]{1,0:T(8,128)(2,1)} %get-tuple-element.32.hid_ref.refs_7_, bf16[4096,896]{1,0:T(8,128)(2,1)} %bitcast.15, bf16[2304,896]{1,0:T(8,128)(2,1)} %get-tuple-element.33.w_ref.refs_11_, bf16[2,288,896]{2,1,0:T(8,128)(2,1)} %wd_ref.3), custom_call_target="tpu_custom_call" | custom-call | flops 16911433728 | bytes 37000000 | tf_op jit(solution)/shard_map/down/pallas_call | solution.py:226
  130.4 127.7 %last_layer.1 = (bf16[4096,2304]{1,0:T(8,128)(2,1)}, bf16[4096,2304]{1,0:T(8,128)(2,1)}, bf16[4096,2304]{1,0:T(8,128)(2,1)}, bf16[896,4096]{1,0:T(8,128)(2,1)}, ...) custom-call(bf16[4096,896]{1,0:T(8,128)(2,1)} %get-tuple-element.34.h_ref, ...), custom_call_target="tpu_custom_call" | custom-call | flops 84557168640 | bytes 110000000 | tf_op jit(solution)/shard_map/last_layer/pallas_call | solution.py:291
  258.1 203.8 %gradients.1 = (bf16[288,896]{1,0:T(8,128)(2,1)}, bf16[112,2304]{1,0:T(8,128)(2,1)}, bf16[112,2304]{1,0:T(8,128)(2,1)}, bf16[288,896]{1,0:T(8,128)(2,1)}, bf16[1...) custom-call(bf16[896,4096]{1,0:T(8,128)(2,1)} %get-tuple-element.38., ...), custom_call_target="tpu_custom_call" | custom-call | flops 118380036096 | bytes 270000000 | tf_op jit(solution)/shard_map/gradients/pallas_call | solution.py:616
  461.9 1.3 reduce_sum.9
  463.9 0.0 copy-start
  463.9 0.0 copy-start.1
  463.9 0.0 copy-start.2
  463.9 0.0 copy-start.3
  464.0 0.0 copy-start.4
  464.0 0.0 copy-start.5
  464.0 0.0 copy-start.6
  464.0 0.0 copy-start.7
  464.0 6.0 %fusion.8 = (bf16[2,288,896]{2,1,0:T(8,128)(2,1)}, f32[2,288,896]{2,1,0:T(8,128)}, f32[2,288,896]{2,1,0:T(8,128)}) fusion(bf16[2,288,896]{2,1,0:T(8,128)(2,1)} %wd_ref.3, f32[]{:T(128)S(6)} %min_shard_map.3, bf16[1,288,896]{2,1,0:T(8,128)(2,1)} %bitcast.12, bf16[1,288,896]{2,1,0:T(8,128)(2,1)} %bitcast.13, f32[2,288,896]{2,1,0:T(8,128)} %param.21, ...), kind=kLoop, calls=%fused_computation.17 | loop fusion | flops 10321920 | bytes 11354116 | tf_op jit(solution)/shard_map/convert_element_type | solution.py:655
  470.0 0.0 copy-done
  470.0 0.0 copy-done.1
  470.0 0.0 copy-done.2
  470.0 1.0 copy-done.3
  471.1 0.2 copy-done.4
  471.3 0.3 copy-done.5
  471.6 0.1 copy-done.6
  471.7 0.1 copy-done.7
  471.8 6.1 %fusion.2 = (bf16[2,112,2304]{2,1,0:T(8,128)(2,1)}, f32[2,112,2304]{2,1,0:T(8,128)}, f32[2,112,2304]{2,1,0:T(8,128)}, bf16[2,112,2304]{2,1,0:T(8,128)(2,1)}, f32...) fusion(bf16[2,112,2304]{2,1,0:T(8,128)(2,1)S(1)} %copy-done.4, f32[]{:T(128)S(6)} %min_shard_map.3, ...), kind=kLoop, calls=%fused_computation.11 | loop fusion | flops 20643840 | bytes 22708228 | tf_op jit(solution)/shard_map/convert_element_type | solution.py:655
Async XLA Ops:
  463.9 6.1 %copy-start = (f32[2,112,2304]{2,1,0:T(8,128)S(1)}, f32[2,112,2304]{2,1,0:T(8,128)}, u32[]{:S(2)}) copy-start(f32[2,112,2304]{2,1,0:T(8,128)} %param.19) | copy-start | bytes 6193156
  463.9 6.1 %copy-start.1 = (f32[2,112,2304]{2,1,0:T(8,128)S(1)}, f32[2,112,2304]{2,1,0:T(8,128)}, u32[]{:S(2)}) copy-start(f32[2,112,2304]{2,1,0:T(8,128)} %param.16) | copy-start | bytes 6193156
  463.9 6.1 %copy-start.2 = (f32[2,112,2304]{2,1,0:T(8,128)S(1)}, f32[2,112,2304]{2,1,0:T(8,128)}, u32[]{:S(2)}) copy-start(f32[2,112,2304]{2,1,0:T(8,128)} %param.20) | copy-start | bytes 6193156
  463.9 7.1 %copy-start.3 = (f32[2,112,2304]{2,1,0:T(8,128)S(1)}, f32[2,112,2304]{2,1,0:T(8,128)}, u32[]{:S(2)}) copy-start(f32[2,112,2304]{2,1,0:T(8,128)} %param.17) | copy-start | bytes 6193156
  464.0 7.3 %copy-start.4 = (bf16[2,112,2304]{2,1,0:T(8,128)(2,1)S(1)}, bf16[2,112,2304]{2,1,0:T(8,128)(2,1)}, u32[]{:S(2)}) copy-start(bf16[2,112,2304]{2,1,0:T(8,128)(2,1)} %wg_ref.1) | copy-start | bytes 3096580
  464.0 7.6 %copy-start.5 = (bf16[2,112,2304]{2,1,0:T(8,128)(2,1)S(1)}, bf16[2,112,2304]{2,1,0:T(8,128)(2,1)}, u32[]{:S(2)}) copy-start(bf16[2,112,2304]{2,1,0:T(8,128)(2,1)} %wu_ref.1) | copy-start | bytes 3096580
  464.0 7.7 %copy-start.6 = (bf16[112,2304]{1,0:T(8,128)(2,1)S(1)}, bf16[112,2304]{1,0:T(8,128)(2,1)}, u32[]{:S(2)}) copy-start(bf16[112,2304]{1,0:T(8,128)(2,1)} %get-tuple-element.49) | copy-start | bytes 1548292
  464.0 7.8 %copy-start.7 = (bf16[112,2304]{1,0:T(8,128)(2,1)S(1)}, bf16[112,2304]{1,0:T(8,128)(2,1)}, u32[]{:S(2)}) copy-start(bf16[112,2304]{1,0:T(8,128)(2,1)} %get-tuple-element.52) | copy-start | bytes 1548292

commit v3 on v2

--- a/solution.py
+++ b/solution.py
@@ -241,37 +241,30 @@
     )(hid, h, w, wd)
 
 
-def last_kernel(h_ref, dy_ref, wg_ref, wu_ref, wd_ref, hid_ref, dg_ref, du_ref, at_ref, dyt_ref, dh_ref, dht_ref, gt, ut, dt):
+def last_kernel(h_ref, dy_ref, wg_ref, wu_ref, wd_ref, hid_ref, dg_ref, du_ref, at_ref, dyt_ref, dh_ref, dht_ref):
     h = wide(h_ref[...])
     scale = scale_of(h)
     a = (h * scale).astype(BF)
     dy = dy_ref[...]
     f = wg_ref.shape[1]
-
-    @pl.when(pl.program_id(0) == 0)
-    def _():
-        for n in range(0, f, 256):
-            where = slice(n, n + 256)
-            gt[where, :] = wg_ref[:, where].T
-            ut[where, :] = wu_ref[:, where].T
-            dt[:, where] = wd_ref[where, :].T
-
     at_ref[...] = a.T
     dyt_ref[...] = dy.T
-    by_a = jnp.zeros(h.shape, F32)
-    for n in range(0, f, 768):
-        for k in range(n, n + 768, 256):
-            where = slice(k, k + 256)
-            g = dot(a, wg_ref[:, where])
-            u = dot(a, wu_ref[:, where])
-            back = wide(dot(dy, dt[:, where]).astype(BF))
-            s = sigmoid(g)
-            silu = g * s
-            hid_ref[:, where] = (silu * u).astype(BF)
-            du_ref[:, where] = (back * silu).astype(BF)
-            dg_ref[:, where] = (back * u * (s * (1.0 + g * (1.0 - s)))).astype(BF)
-        where = slice(n, n + 768)
-        by_a += dot(dg_ref[:, where], gt[where, :]) + dot(du_ref[:, where], ut[where, :])
+    for k in range(0, f, 256):
+        where = slice(k, k + 256)
+        g = dot(a, wg_ref[:, where])
+        u = dot(a, wu_ref[:, where])
+        back = wide(dot(dy, wd_ref[where, :], ((1,), (1,))).astype(BF))
+        s = sigmoid(g)
+        silu = g * s
+        hid_ref[:, where] = (silu * u).astype(BF)
+        du_ref[:, where] = (back * silu).astype(BF)
+        dg_ref[:, where] = (back * u * (s * (1.0 + g * (1.0 - s)))).astype(BF)
+    d = h.shape[1]
+    parts = []
+    for k in range(0, d, 256):
+        rows = slice(k, min(k + 256, d))
+        parts.append(dot(dg_ref[...], wg_ref[rows, :], ((1,), (1,))) + dot(du_ref[...], wu_ref[rows, :], ((1,), (1,))))
+    by_a = jnp.concatenate(parts, 1)
     by_a = wide(by_a.astype(BF))
     mean = jnp.mean(by_a * h, -1, keepdims=True)
     by_h = (by_a * scale - h * (scale * scale * scale * mean)).astype(BF)
@@ -294,7 +287,6 @@
         out_shape=[shape(tokens, f)] * 3 + [shape(d, tokens)] * 2 + [shape(tokens, d), shape(d, tokens)],
         in_specs=[rows(d), rows(d), fixed(d, f), fixed(d, f), fixed(f, d)],
         out_specs=[rows(f)] * 3 + [columns] * 2 + [rows(d), columns],
-        scratch_shapes=[pltpu.VMEM((f, d), BF)] * 2 + [pltpu.VMEM((d, f), BF)],
         compiler_params=pltpu.CompilerParams(vmem_limit_bytes=LIMIT, dimension_semantics=("arbitrary",)),
         cost_estimate=pl.CostEstimate(flops=10 * tokens * d * f, bytes_accessed=110_000_000, transcendentals=tokens * f),
         name="last_layer",
@@ -457,7 +449,7 @@
         return pl.ds(n * CHUNK, CHUNK), pl.ds(pl.multiple_of(i * TILE, TILE), TILE)
 
     def load_chunk(n, i, slot):
-        rows, cols = chunk_at(n, i)
+        rows, cols = pl.ds(pl.multiple_of(n * CHUNK, CHUNK), CHUNK), chunk_at(0, i)[1]
         pairs = [(gate.at[rows, cols], in_vmem.at[slot, 0]), (up.at[rows, cols], in_vmem.at[slot, 1])]
         copies = [pltpu.make_async_copy(a, b, in_sem.at[slot, k]) for k, (a, b) in enumerate(pairs)]
         return [*copies, pltpu.make_async_copy(down.at[cols], w_vmem.at[slot], w_sem.at[slot])]
@@ -515,6 +507,9 @@
                 sg = sigmoid(g)
                 out_vmem[slot, 0] = (back * u * (sg * (1.0 + g * (1.0 - sg)))).astype(BF)
                 out_vmem[slot, 1] = (back * (g * sg)).astype(BF)
+                if n + 1 < chunks:
+                    after = n * tiles + i + slots
+                    do(load_chunk(after // tiles, after % tiles, slot), "start")
             total = dot(left[which % 2], right[slot])
             where = pl.ds(pl.multiple_of(i * TILE, TILE), TILE)
             if turned:
@@ -528,7 +523,7 @@
             @pl.when(i + slots < tiles)
             def _():
                 load_right(n, i + slots, slot).start()
-                if n < chunks:
+                if n + 1 == chunks:
                     do(load_chunk(n, i + slots, slot), "start")
 
             if n + 1 < len(phases):
@@ -536,8 +531,6 @@
                 @pl.when(i + slots >= tiles)
                 def _():
                     load_right(n + 1, i + slots - tiles, slot).start()
-                    if n + 1 < chunks:
-                        do(load_chunk(n + 1, i + slots - tiles, slot), "start")
 
             return carry
 

time: 483 us -> 464 us (0.961)
  Pallas kernels: 461 us -> 447 us
    pallas_call x1, Pallas kernels: 128 us -> 115 us  [last_layer(): pl.pallas_call(last_kernel, grid=(tokens // tile,), out_shape=[shape(toke...]
where the time goes in v3:
time: 464 us
  Pallas kernels  447 us (96%)
  other arithmetic  13.4 us (3%)
    pallas_call x1, Pallas kernels, gradients(): pl.pallas_call(functools.partial(gradients_kernel, phases, pieces, tiles)...  203 us
    pallas_call x1, Pallas kernels, last_layer(): pl.pallas_call(last_kernel, grid=(tokens // tile,), out_shape=[shape(toke...  115 us
    pallas_call x1, Pallas kernels, gate_up(): pl.pallas_call(functools.partial(gate_up_kernel, parts, tiles), grid=(par...  95.2 us
    pallas_call x1, Pallas kernels, down(): pl.pallas_call(functools.partial(down_kernel, tokens // tile), grid=(toke...  34.5 us
    convert_element_type x2, other arithmetic, adamw(): return ((w - 0.02 * step).astype(jnp.bfloat16), m, v)  12.2 us

profile of v3, /device:TPU:0, one launch (start us, length us, event | category | flops | bytes accessed | tf_op | source)
XLA Modules:
  0.0 463.7 jit_solution(17453657121563588790)
XLA Ops:
  0.6 95.2 %gate_up.1 = (f32[4096,2304]{1,0:T(8,128)}, f32[4096,2304]{1,0:T(8,128)}, bf16[4096,2304]{1,0:T(8,128)(2,1)}, bf16[896,4096]{1,0:T(8,128)(2,1)}, bf16[2304,896]{...) custom-call(bf16[4096,896]{1,0:T(8,128)(2,1)} %bitcast.14, bf16[2,112,2304]{2,1,0:T(8,128)(2,1)} %wg_ref.1, ...), custom_call_target="tpu_custom_call" | custom-call | flops 33822867456 | bytes 110000000 | tf_op jit(solution)/shard_map/gate_up/pallas_call | solution.py:181
  95.9 34.5 %down.1 = (bf16[4096,896]{1,0:T(8,128)(2,1)}, bf16[2304,896]{1,0:T(8,128)(2,1)}) custom-call(bf16[4096,2304]{1,0:T(8,128)(2,1)} %get-tuple-element.32.hid_ref.refs_7_, bf16[4096,896]{1,0:T(8,128)(2,1)} %bitcast.15, bf16[2304,896]{1,0:T(8,128)(2,1)} %get-tuple-element.33.w_ref.refs_11_, bf16[2,288,896]{2,1,0:T(8,128)(2,1)} %wd_ref.3), custom_call_target="tpu_custom_call" | custom-call | flops 16911433728 | bytes 37000000 | tf_op jit(solution)/shard_map/down/pallas_call | solution.py:226
  130.4 114.8 %last_layer.1 = (bf16[4096,2304]{1,0:T(8,128)(2,1)}, bf16[4096,2304]{1,0:T(8,128)(2,1)}, bf16[4096,2304]{1,0:T(8,128)(2,1)}, bf16[896,4096]{1,0:T(8,128)(2,1)}, ...) custom-call(bf16[4096,896]{1,0:T(8,128)(2,1)} %get-tuple-element.34.h_ref, ...), custom_call_target="tpu_custom_call" | custom-call | flops 84557168640 | bytes 110000000 | tf_op jit(solution)/shard_map/last_layer/pallas_call | solution.py:284
  245.2 202.6 %gradients.1 = (bf16[288,896]{1,0:T(8,128)(2,1)}, bf16[112,2304]{1,0:T(8,128)(2,1)}, bf16[112,2304]{1,0:T(8,128)(2,1)}, bf16[288,896]{1,0:T(8,128)(2,1)}, bf16[1...) custom-call(bf16[896,4096]{1,0:T(8,128)(2,1)} %get-tuple-element.38., ...), custom_call_target="tpu_custom_call" | custom-call | flops 118380036096 | bytes 270000000 | tf_op jit(solution)/shard_map/gradients/pallas_call | solution.py:609
  447.7 1.3 reduce_sum.9
  449.7 0.0 copy-start
  449.7 0.0 copy-start.1
  449.7 0.0 copy-start.2
  449.7 0.0 copy-start.3
  449.8 0.0 copy-start.4
  449.8 0.0 copy-start.5
  449.8 0.0 copy-start.6
  449.8 0.0 copy-start.7
  449.8 6.0 %fusion.8 = (bf16[2,288,896]{2,1,0:T(8,128)(2,1)}, f32[2,288,896]{2,1,0:T(8,128)}, f32[2,288,896]{2,1,0:T(8,128)}) fusion(bf16[2,288,896]{2,1,0:T(8,128)(2,1)} %wd_ref.3, f32[]{:T(128)S(6)} %min_shard_map.3, bf16[1,288,896]{2,1,0:T(8,128)(2,1)} %bitcast.12, bf16[1,288,896]{2,1,0:T(8,128)(2,1)} %bitcast.13, f32[2,288,896]{2,1,0:T(8,128)} %param.21, ...), kind=kLoop, calls=%fused_computation.17 | loop fusion | flops 10321920 | bytes 11354116 | tf_op jit(solution)/shard_map/convert_element_type | solution.py:648
  455.8 0.0 copy-done
  455.8 0.0 copy-done.1
  455.8 0.0 copy-done.2
  455.8 1.0 copy-done.3
  456.8 0.2 copy-done.4
  457.1 0.3 copy-done.5
  457.4 0.1 copy-done.6
  457.5 0.1 copy-done.7
  457.6 6.1 %fusion.2 = (bf16[2,112,2304]{2,1,0:T(8,128)(2,1)}, f32[2,112,2304]{2,1,0:T(8,128)}, f32[2,112,2304]{2,1,0:T(8,128)}, bf16[2,112,2304]{2,1,0:T(8,128)(2,1)}, f32...) fusion(bf16[2,112,2304]{2,1,0:T(8,128)(2,1)S(1)} %copy-done.4, f32[]{:T(128)S(6)} %min_shard_map.3, ...), kind=kLoop, calls=%fused_computation.11 | loop fusion | flops 20643840 | bytes 22708228 | tf_op jit(solution)/shard_map/convert_element_type | solution.py:648
Async XLA Ops:
  449.7 6.1 %copy-start = (f32[2,112,2304]{2,1,0:T(8,128)S(1)}, f32[2,112,2304]{2,1,0:T(8,128)}, u32[]{:S(2)}) copy-start(f32[2,112,2304]{2,1,0:T(8,128)} %param.19) | copy-start | bytes 6193156
  449.7 6.1 %copy-start.1 = (f32[2,112,2304]{2,1,0:T(8,128)S(1)}, f32[2,112,2304]{2,1,0:T(8,128)}, u32[]{:S(2)}) copy-start(f32[2,112,2304]{2,1,0:T(8,128)} %param.16) | copy-start | bytes 6193156
  449.7 6.1 %copy-start.2 = (f32[2,112,2304]{2,1,0:T(8,128)S(1)}, f32[2,112,2304]{2,1,0:T(8,128)}, u32[]{:S(2)}) copy-start(f32[2,112,2304]{2,1,0:T(8,128)} %param.20) | copy-start | bytes 6193156
  449.7 7.1 %copy-start.3 = (f32[2,112,2304]{2,1,0:T(8,128)S(1)}, f32[2,112,2304]{2,1,0:T(8,128)}, u32[]{:S(2)}) copy-start(f32[2,112,2304]{2,1,0:T(8,128)} %param.17) | copy-start | bytes 6193156
  449.8 7.3 %copy-start.4 = (bf16[2,112,2304]{2,1,0:T(8,128)(2,1)S(1)}, bf16[2,112,2304]{2,1,0:T(8,128)(2,1)}, u32[]{:S(2)}) copy-start(bf16[2,112,2304]{2,1,0:T(8,128)(2,1)} %wg_ref.1) | copy-start | bytes 3096580
  449.8 7.6 %copy-start.5 = (bf16[2,112,2304]{2,1,0:T(8,128)(2,1)S(1)}, bf16[2,112,2304]{2,1,0:T(8,128)(2,1)}, u32[]{:S(2)}) copy-start(bf16[2,112,2304]{2,1,0:T(8,128)(2,1)} %wu_ref.1) | copy-start | bytes 3096580
  449.8 7.7 %copy-start.6 = (bf16[112,2304]{1,0:T(8,128)(2,1)S(1)}, bf16[112,2304]{1,0:T(8,128)(2,1)}, u32[]{:S(2)}) copy-start(bf16[112,2304]{1,0:T(8,128)(2,1)} %get-tuple-element.49) | copy-start | bytes 1548292
  449.8 7.8 %copy-start.7 = (bf16[112,2304]{1,0:T(8,128)(2,1)S(1)}, bf16[112,2304]{1,0:T(8,128)(2,1)}, u32[]{:S(2)}) copy-start(bf16[112,2304]{1,0:T(8,128)(2,1)} %get-tuple-element.52) | copy-start | bytes 1548292
